TPU v7x, 32 devices: a whole 2x2x4 slice. The times are simulated.
32 devices in a mesh: lat: 4 (over z), lon: 8 (over y, x, core).
Axes of the slice: x: 2, y: 2, z: 4, core: 2. Of those that a mesh axis runs over, the one named last changes fastest.
Arguments:
- inputs: bfloat16 [4, 32, 256, 800], P(None, 'lat', 'lon'), may hold values from -6 to 6
- conv_kernel: bfloat16 [7, 7, 800], replicated, may hold values from -0.875 to 0.875
- norm_gain: bfloat16 [800], replicated, may hold values from 0.5 to 1.5
- norm_shift: bfloat16 [800], replicated, may hold values from -3 to 3
- w_in: bfloat16 [800, 3200], replicated, may hold values from -0.21875 to 0.21875
- b_in: bfloat16 [3200], replicated, may hold values from -3 to 3
- w_out: bfloat16 [3200, 800], replicated, may hold values from -0.109375 to 0.109375
- b_out: bfloat16 [800], replicated, may hold values from -3 to 3
- ocean_mask: int32 [32, 256], P('lat', 'lon'), may hold values from 0 to 1, as said below
- lengths: int32 [4], replicated, may hold values from 1 to 8, as said below
- cotangent: bfloat16 [4, 32, 256, 800], P(None, 'lat', 'lon'), may hold values from -6 to 6
Outputs:
- output: bfloat16 [4, 32, 256, 800], P(None, 'lat', 'lon')
- d_inputs: bfloat16 [4, 32, 256, 800], P(None, 'lat', 'lon')
- d_kernel: float32 [7, 7, 800], replicated
- d_gain: float32 [800], replicated
- d_shift: float32 [800], replicated
- d_w_in: float32 [800, 3200], replicated
- d_b_in: float32 [3200], replicated
- d_w_out: float32 [3200, 800], replicated
- d_b_out: float32 [800], replicated
Inputs may be any that keep to these rules, and one draw needn't show every extreme that they name: `ocean_mask`: a 0/1 mask; the last latitude row is all ocean. `lengths`: some micro-batch completes the whole rollout.
All inputs are finite; a program needn't handle non-finite values.
Results may differ from a plain program's by a relative error of at most 0.0063.
Values may be sent and summed in bfloat16 or wider, within the bound.
A program may use at most 128 MiB of HBM per device.

v0:
```python
import jax
import jax.numpy as jnp
from jax import lax
from jax.sharding import PartitionSpec as P

KS = 7
ROLLOUT = 8
epsilon = 1e-05


def with_halo(value, sides, width):
    for axis, dim in sides:
        count, length = (lax.axis_size(axis), value.shape[dim])
        up = [(i, (i + 1) % count) for i in range(count - 1)]
        down = [(j, i) for i, j in up]
        last = lax.slice_in_dim(value, length - width, length, axis=dim)
        initial = lax.slice_in_dim(value, 0, width, axis=dim)
        before = lax.ppermute(last, axis, up)
        after = lax.ppermute(initial, axis, down)
        value = jnp.concatenate([before, value, after], axis=dim)
    return value


def smooth_gate(values):
    return jax.nn.gelu(values, approximate=True)


def body(
    inputs,
    conv_kernel,
    norm_gain,
    norm_shift,
    w_in,
    b_in,
    w_out,
    b_out,
    ocean_mask,
    lengths,
    cotangent,
):
    batches, tile_rows, tile_cols, channels = inputs.shape
    half_side = KS // 2
    padded = with_halo(inputs, (("lat", 1), ("lon", 2)), half_side).astype(jnp.float32)
    kernel = conv_kernel.astype(jnp.float32)
    convolved = jnp.zeros(inputs.shape, jnp.float32)
    for row_shift in range(KS):
        for col_shift in range(KS):
            convolved = (
                convolved
                + kernel[row_shift, col_shift]
                * padded[:, row_shift : row_shift + tile_rows, col_shift : col_shift + tile_cols]
            )
    ocean_cells = ocean_mask.astype(jnp.float32)[None, :, :, None]
    local_count = jnp.sum(ocean_mask).astype(jnp.float32) * batches
    masked = convolved * ocean_cells
    sum_cells, cell_count = lax.psum((jnp.sum(masked, axis=(0, 1, 2)), local_count), ("lat", "lon"))
    mean_value = sum_cells / cell_count
    centered = convolved - mean_value
    variance = (
        lax.psum(jnp.sum(centered * centered * ocean_cells, axis=(0, 1, 2)), ("lat", "lon"))
        / cell_count
    )
    inv_std = lax.rsqrt(variance + epsilon)
    standard = centered * inv_std
    gain_vec = norm_gain.astype(jnp.float32)
    normed = (
        (standard * gain_vec + norm_shift.astype(jnp.float32))
        .astype(jnp.bfloat16)
        .reshape(-1, channels)
    )
    pre_gate = jnp.dot(normed, w_in, preferred_element_type=jnp.float32) + b_in.astype(jnp.float32)
    activated, gate_back = jax.vjp(smooth_gate, pre_gate)
    act_low = activated.astype(jnp.bfloat16)
    branch = jnp.dot(act_low, w_out, preferred_element_type=jnp.float32) + b_out.astype(jnp.float32)
    output = (inputs.astype(jnp.float32) + ocean_cells * branch.reshape(inputs.shape)).astype(
        jnp.bfloat16
    )
    kept_steps = lengths.astype(jnp.float32) / ROLLOUT
    d_output = cotangent.astype(jnp.float32) * kept_steps[:, None, None, None]
    d_branch = (d_output * ocean_cells).reshape(-1, channels)
    branch_low = d_branch.astype(jnp.bfloat16)
    local_b_out = jnp.sum(d_branch, axis=0)
    local_w_out = lax.dot_general(
        act_low, branch_low, (((0,), (0,)), ((), ())), preferred_element_type=jnp.float32
    )
    d_act = lax.dot_general(
        branch_low, w_out, (((1,), (1,)), ((), ())), preferred_element_type=jnp.float32
    )
    d_pre = gate_back(d_act)[0]
    pre_low = d_pre.astype(jnp.bfloat16)
    local_b_in = jnp.sum(d_pre, axis=0)
    local_w_in = lax.dot_general(
        normed, pre_low, (((0,), (0,)), ((), ())), preferred_element_type=jnp.float32
    )
    d_normed = lax.dot_general(
        pre_low, w_in, (((1,), (1,)), ((), ())), preferred_element_type=jnp.float32
    ).reshape(inputs.shape)
    d_shift, d_gain = lax.psum(
        (jnp.sum(d_normed, axis=(0, 1, 2)), jnp.sum(d_normed * standard, axis=(0, 1, 2))),
        ("lat", "lon"),
    )
    d_conv = (
        gain_vec * inv_std * (d_normed - ocean_cells * (d_shift + standard * d_gain) / cell_count)
    )
    conv_low = d_conv.astype(jnp.bfloat16)
    conv_back = conv_low.astype(jnp.float32)
    d_padded = with_halo(conv_low, (("lat", 1), ("lon", 2)), half_side).astype(jnp.float32)
    d_inputs = d_output
    kernel_rows = []
    for row_shift in range(KS):
        kernel_cols = []
        for col_shift in range(KS):
            top_edge = 2 * half_side - row_shift
            left_edge = 2 * half_side - col_shift
            d_inputs = (
                d_inputs
                + kernel[row_shift, col_shift]
                * d_padded[:, top_edge : top_edge + tile_rows, left_edge : left_edge + tile_cols]
            )
            kernel_cols.append(
                jnp.sum(
                    padded[:, row_shift : row_shift + tile_rows, col_shift : col_shift + tile_cols]
                    * conv_back,
                    axis=(0, 1, 2),
                )
            )
        kernel_rows.append(jnp.stack(kernel_cols, axis=0))
    local_kernel = jnp.stack(kernel_rows, axis=0)
    d_w_in, d_b_in, d_w_out, d_b_out, d_kernel = lax.psum(
        (local_w_in, local_b_in, local_w_out, local_b_out, local_kernel), ("lat", "lon")
    )
    return (
        output,
        d_inputs.astype(jnp.bfloat16),
        d_kernel,
        d_gain,
        d_shift,
        d_w_in,
        d_b_in,
        d_w_out,
        d_b_out,
    )


def solution(mesh):
    in_specs = (
        P(None, "lat", "lon", None),
        P(),
        P(),
        P(),
        P(),
        P(),
        P(),
        P(),
        P("lat", "lon"),
        P(),
        P(None, "lat", "lon", None),
    )
    out_specs = (
        P(None, "lat", "lon", None),
        P(None, "lat", "lon", None),
        P(),
        P(),
        P(),
        P(),
        P(),
        P(),
        P(),
    )
    return jax.shard_map(body, mesh=mesh, in_specs=in_specs, out_specs=out_specs, check_vma=False)
```

profile of v0, /device:TPU:0, one launch (start us, length us, event | category | flops | bytes accessed | tf_op | source)
XLA Modules:
  0.0 802.5 jit_solution(7980554916226600556)
XLA Ops:
  7.2 1.5 fusion.116
  8.8 5.0 collective-permute-start
  13.8 1.3 collective-permute-start.1
  15.1 0.9 convert_element_type.65
  16.8 1.4 fusion.117
  18.2 10.2 %collective-permute-done = bf16[4,3,32,800]{3,2,1,0:T(8,128)(2,1)S(1)} collective-permute-done((bf16[4,3,32,800]{3,2,1,0:T(8,128)(2,1)S(1)}, bf16[4,3,32,800]{3,2,1,0:T(8,128)(2,1)S(1)}, u32[]{:S(2)}, u32[]{:S(2)}) %collective-permute-start) | collective-permute-done | bytes 614432 | tf_op jit(solution)/shard_map/ppermute | solution.py:18
  28.9 3.7 collective-permute-done.1
  32.7 1.7 copy-done.3
  34.7 1.3 collective-permute-start.3
  36.0 3.1 collective-permute-start.2
  39.1 0.7 slice_reduce_fusion.46
  40.5 0.6 convert_multiply_fusion.51
  41.1 5.5 maximum_convert_fusion
  47.0 83.2 %multiply_reduce_fusion.2 = (f32[800]{0:T(1024)S(1)}, f32[4,8,32,800]{3,2,1,0:T(8,128)}) fusion(f32[8,32]{1,0:T(8,128)S(1)} %get-tuple-element.136, f32[4,14,38,800]{3,2,1,0:T(8,128)} %maximum_convert_fusion, f32[800]{0:T(1024)S(1)} %get-tuple-element.59, f32[800]{0:T(1024)S(1)} %get-tuple-element.60, f32[800]{0:T(1024)S(1)} %get-tuple-element.61, ...), kind=kLoop, calls=%fused_computation.217 | loop fusion | flops 81100000 | bytes 164001024 | tf_op jit(solution)/shard_map/reduce_sum | solution.py:56
  130.2 46.7 %all-reduce.1 = (f32[800]{0:T(1024)S(1)}, f32[]{:T(128)}) all-reduce(f32[800]{0:T(1024)S(1)} %get-tuple-element.123, f32[]{:T(128)S(6)} %mul.1208), channel_id=1, replica_groups=mesh['lat'=4,'lon'=8] {'lat','lon'}, use_global_device_ids=true, to_apply=%region_1.0 | all-reduce | flops 801 | bytes 6408 | tf_op jit(solution)/shard_map/psum | solution.py:56
  176.9 0.6 broadcast_divide_fusion
  177.6 4.4 fusion.106
  182.0 40.0 %psum.72 = f32[800]{0:T(1024)S(1)} all-reduce(f32[800]{0:T(1024)S(1)} %get-tuple-element.108), channel_id=1, replica_groups=mesh['lat'=4,'lon'=8] {'lat','lon'}, use_global_device_ids=true, to_apply=%region_5.0 | all-reduce | flops 800 | bytes 6400 | tf_op jit(solution)/shard_map/psum | solution.py:60
  222.0 0.7 convert_multiply_fusion.50
  222.7 2.8 add_convert_fusion.1
  225.5 13.3 %fusion.119 = f32[1024,3200]{1,0:T(8,128)} fusion(bf16[1024,800]{1,0:T(8,128)(2,1)S(1)} %bitcast.38, bf16[800,3200]{1,0:T(8,128)(2,1)} %param.15), kind=kOutput, calls=%fused_computation.297 | convolution fusion | flops 5242880000 | bytes 19865600 | tf_op jit(solution)/shard_map/dot_general | solution.py:71
  238.8 16.8 %fusion.112 = (f32[3200]{0:T(1024)S(1)}, bf16[1024,3200]{1,0:T(8,128)(2,1)}, bf16[1024,3200]{1,0:T(8,128)(2,1)}) fusion(f32[1024,3200]{1,0:T(8,128)} %fusion.119, f32[3200]{0:T(1024)S(1)} %convert_element_type.71, bf16[1024,800]{1,0:T(8,128)(2,1)S(1)} %bitcast.37, bf16[3200,800]{0,1:T(8,128)(2,1)S(1)} %bitcast.43), kind=kOutput, calls=%fused_computation.291 | convolution fusion | flops 5321520128 | bytes 32998400 | tf_op jit(solution)/shard_map/dot_general | solution.py:86
  255.6 9.1 %fusion.118 = (f32[800]{0:T(1024)S(1)}, f32[1024,800]{0,1:T(8,128)}) fusion(bf16[800,3200]{1,0:T(8,128)(2,1)S(1)} %bitcast.41, bf16[1024,3200]{1,0:T(8,128)(2,1)} %get-tuple-element.122), kind=kOutput, calls=%fused_computation.296 | convolution fusion | flops 5243698176 | bytes 14953600 | tf_op jit(solution)/shard_map/dot_general | solution.py:95
  264.8 4.9 copy.24
  269.6 3.8 multiply_reduce_fusion
  273.4 41.2 %all-reduce = (f32[800]{0:T(1024)S(1)}, f32[800]{0:T(1024)S(1)}, f32[3200]{0:T(1024)}, f32[800]{0:T(1024)}) all-reduce(f32[800]{0:T(1024)S(1)} %multiply_reduce_fusion, f32[800]{0:T(1024)S(1)} %get-tuple-element.137, f32[3200]{0:T(1024)S(1)} %get-tuple-element.121, ...), channel_id=1, replica_groups=mesh['lat'=4,'lon'=8] {'lat','lon'}, use_global_device_ids=true, to_apply=%region_9.0 | all-reduce | flops 5600 | bytes 44800 | tf_op jit(solution)/shard_map/psum | solution.py:98
  314.7 36.2 %fusion.53 = (f32[800]{0:T(1024)S(1)}, f32[800]{0:T(1024)S(1)}, f32[800]{0:T(1024)S(1)}, f32[800]{0:T(1024)S(1)}, f32[800]{0:T(1024)S(1)}, /*index=5*/f32[800]{0...) fusion(f32[4,14,38,800]{3,2,1,0:T(8,128)} %maximum_convert_fusi, ...), kind=kLoop, calls=%fused_computation.107 | loop fusion | flops 37668800 | bytes 67249024 | tf_op jit(solution)/shard_map/reduce_sum | solution.py:121
  350.9 22.8 %fusion.52 = (f32[800]{0:T(1024)S(1)}, f32[800]{0:T(1024)S(1)}, f32[800]{0:T(1024)S(1)}, f32[800]{0:T(1024)S(1)}, f32[800]{0:T(1024)S(1)}, /*index=5*/f32[800]{0...) fusion(bf16[4,8,32,800]{3,2,1,0:T(8,128)(2,1)S(1)} %get-tuple-e, ...), kind=kLoop, calls=%fused_computation.106 | loop fusion | flops 22108000 | bytes 44278400 | tf_op jit(solution)/shard_map/reduce_sum | solution.py:121
  373.7 40.0 %fusion.54 = (f32[800]{0:T(1024)S(1)}, f32[800]{0:T(1024)S(1)}, f32[800]{0:T(1024)S(1)}, f32[800]{0:T(1024)S(1)}, f32[800]{0:T(1024)S(1)}, /*index=5*/f32[800]{0...) fusion(bf16[4,8,32,800]{3,2,1,0:T(8,128)(2,1)S(1)} %get-tuple-e, ...), kind=kLoop, calls=%fused_computation.108 | loop fusion | flops 30296000 | bytes 60678400 | tf_op jit(solution)/shard_map/reduce_sum | solution.py:121
  413.7 12.6 %fusion.108 = f32[800,3200]{1,0:T(8,128)} fusion(bf16[1024,800]{1,0:T(8,128)(2,1)S(1)} %bitcast.39, bf16[1024,3200]{1,0:T(8,128)(2,1)} %get-tuple-element.122), kind=kOutput, calls=%fused_computation.220 | convolution fusion | flops 5242880000 | bytes 18432000 | tf_op jit(solution)/shard_map/dot_general | solution.py:92
  427.0 13.1 %fusion.120 = f32[3200,800]{0,1:T(8,128)} fusion(bf16[1024,3200]{1,0:T(8,128)(2,1)} %get-tuple-element.125, bf16[1024,800]{1,0:T(8,128)(2,1)} %bitcast.36), kind=kOutput, calls=%fused_computation.298 | convolution fusion | flops 5242880000 | bytes 18432000 | tf_op jit(solution)/shard_map/dot_general | solution.py:83
  440.5 0.7 copy-done.7
  441.2 1.4 fusion.115
  442.6 1.3 collective-permute-start.5
  443.9 4.6 collective-permute-start.4
  448.5 11.0 %convolution_add_fusion = f32[1024,800]{0,1:T(8,128)} fusion(bf16[1024,3200]{1,0:T(8,128)(2,1)} %get-tuple-element.125, bf16[3200,800]{0,1:T(8,128)(2,1)} %param.17, f32[800]{0:T(1024)S(1)} %convert_element_type.73), kind=kOutput, calls=%fused_computation.224 | convolution fusion | flops 5243699200 | bytes 14953600 | tf_op jit(solution)/shard_map/dot_general | solution.py:74
  459.5 4.9 copy.23
  464.4 10.1 %collective-permute-done.5 = bf16[4,3,32,800]{3,2,1,0:T(8,128)(2,1)S(1)} collective-permute-done((bf16[4,3,32,800]{3,2,1,0:T(8,128)(2,1)}, bf16[4,3,32,800]{3,2,1,0:T(8,128)(2,1)S(1)}, u32[]{:S(2)}, u32[]{:S(2)}) %collective-permute-start.5) | collective-permute-done | bytes 614432 | tf_op jit(solution)/shard_map/ppermute | solution.py:19
  474.5 4.1 collective-permute-done.4
  478.9 1.3 collective-permute-start.7
  480.2 3.1 collective-permute-start.6
  483.3 3.5 add_convert_fusion
  487.1 4.2 maximum_convert_fusion.1
  491.8 104.8 %fusion.56 = bf16[4,8,32,800]{3,2,1,0:T(8,128)(2,1)} fusion(f32[4,14,38,800]{3,2,1,0:T(8,128)} %maximum_convert_fusion.1, bf16[4,8,32,800]{3,2,1,0:T(8,128)(2,1)} %param.21, f32[4]{0:T(128)} %convert_multiply_fusion.51, f32[800]{0:T(1024)S(1)} %copy-done.11, f32[800]{0:T(1024)S(1)} %copy-done.13, f32[800]{0:T(1024)S(1)} %copy-done.15, ...), kind=kLoop, calls=%fused_computation.111 | loop fusion | flops 82739200 | bytes 163996816 | tf_op jit(solution)/shard_map/convert_element_type | solution.py:134
  596.6 184.4 %all-reduce.5.cloned.1.call-done = (f32[7,7,800]{2,1,0:T(8,128)}, f32[800,3200]{1,0:T(8,128)}, f32[3200,800]{0,1:T(8,128)}) async-done(((f32[7,7,800]{2,1,0:T(8,128)}, f32[800,3200]{1,0:T(8,128)}, f32[3200,800]{0,1:T(8,128)}), (f32[7,7,800]{2,1,0:T(8,128)}, f32[800,3200]{1,0:T(8,128)}, f32[3200,800]{0,1:T(8,128)})) %all-reduce.5.cloned.1.call-update) | async-done | bytes 20636816 | tf_op jit(solution)/shard_map/psum | solution.py:129
  781.0 1.8 copy.36
  782.8 8.7 %copy.37 = f32[800,3200]{1,0:T(8,128)} copy(f32[800,3200]{1,0:T(8,128)} %get-tuple-element.147) | data formatting | bytes 20480000
  791.5 4.0 copy.38
  (281 shorter events, 2.7 us)
Async XLA Ops:
  7.2 773.8 %all-reduce.5.cloned.1.call-start = ((), (), s32[]{:S(2)}) async-start(), calls=%async_computation | async-start | bytes 41361408 | tf_op jit(solution)/shard_map/psum | solution.py:129
  8.8 19.6 %collective-permute-start = (bf16[4,3,32,800]{3,2,1,0:T(8,128)(2,1)S(1)}, bf16[4,3,32,800]{3,2,1,0:T(8,128)(2,1)S(1)}, u32[]{:S(2)}, u32[]{:S(2)}) collective-permute-start(bf16[4,3,32,800]{3,2,1,0:T(8,128)(2,1)S(1)} %get-tuple-element.134), channel_id=1, source_target_pairs={{0,8},{8,16},{16,24},{1,9},{9,17},{17,25},{2,10},{10,18},{18,26},{... | collective-permute-start | bytes 1843208 | tf_op jit(solution)/shard_map/ppermute | solution.py:18
  13.8 18.8 %collective-permute-start.1 = (bf16[4,3,32,800]{3,2,1,0:T(8,128)(2,1)S(1)}, bf16[4,3,32,800]{3,2,1,0:T(8,128)(2,1)S(1)}, u32[]{:S(2)}, u32[]{:S(2)}) collective-permute-start(bf16[4,3,32,800]{3,2,1,0:T(8,128)(2,1)S(1)} %get-tuple-element.133), channel_id=1, source_target_pairs={{8,0},{16,8},{24,16},{9,1},{17,9},{25,17},{10,2},{18,10},{26,18},{... | collective-permute-start | bytes 1843208 | tf_op jit(solution)/shard_map/ppermute | solution.py:19
  16.2 30.4 %copy-start.8 = (f32[800]{0:T(1024)}, f32[800]{0:T(1024)S(1)}, u32[]{:S(2)}) copy-start(f32[800]{0:T(1024)S(1)} %get-tuple-element.58) | copy-start | bytes 9604
  16.2 30.4 %copy-start.10 = (f32[800]{0:T(1024)}, f32[800]{0:T(1024)S(1)}, u32[]{:S(2)}) copy-start(f32[800]{0:T(1024)S(1)} %get-tuple-element.59) | copy-start | bytes 9604
  16.2 30.4 %copy-start.12 = (f32[800]{0:T(1024)}, f32[800]{0:T(1024)S(1)}, u32[]{:S(2)}) copy-start(f32[800]{0:T(1024)S(1)} %get-tuple-element.60) | copy-start | bytes 9604
  16.2 30.4 %copy-start.14 = (f32[800]{0:T(1024)}, f32[800]{0:T(1024)S(1)}, u32[]{:S(2)}) copy-start(f32[800]{0:T(1024)S(1)} %get-tuple-element.61) | copy-start | bytes 9604
  16.2 30.4 %copy-start.16 = (f32[800]{0:T(1024)}, f32[800]{0:T(1024)S(1)}, u32[]{:S(2)}) copy-start(f32[800]{0:T(1024)S(1)} %get-tuple-element.62) | copy-start | bytes 9604
  16.2 30.4 %copy-start.18 = (f32[800]{0:T(1024)}, f32[800]{0:T(1024)S(1)}, u32[]{:S(2)}) copy-start(f32[800]{0:T(1024)S(1)} %get-tuple-element.63) | copy-start | bytes 9604
  16.3 30.4 %copy-start.20 = (f32[800]{0:T(1024)}, f32[800]{0:T(1024)S(1)}, u32[]{:S(2)}) copy-start(f32[800]{0:T(1024)S(1)} %get-tuple-element.64) | copy-start | bytes 9604
  16.3 30.4 %copy-start.22 = (f32[800]{0:T(1024)}, f32[800]{0:T(1024)S(1)}, u32[]{:S(2)}) copy-start(f32[800]{0:T(1024)S(1)} %get-tuple-element.65) | copy-start | bytes 9604
  16.3 30.4 %copy-start.24 = (f32[800]{0:T(1024)}, f32[800]{0:T(1024)S(1)}, u32[]{:S(2)}) copy-start(f32[800]{0:T(1024)S(1)} %get-tuple-element.66) | copy-start | bytes 9604
  16.3 30.4 %copy-start.26 = (f32[800]{0:T(1024)}, f32[800]{0:T(1024)S(1)}, u32[]{:S(2)}) copy-start(f32[800]{0:T(1024)S(1)} %get-tuple-element.67) | copy-start | bytes 9604
  16.3 30.4 %copy-start.28 = (f32[800]{0:T(1024)}, f32[800]{0:T(1024)S(1)}, u32[]{:S(2)}) copy-start(f32[800]{0:T(1024)S(1)} %get-tuple-element.68) | copy-start | bytes 9604
  16.3 30.4 %copy-start.30 = (f32[800]{0:T(1024)}, f32[800]{0:T(1024)S(1)}, u32[]{:S(2)}) copy-start(f32[800]{0:T(1024)S(1)} %get-tuple-element.69) | copy-start | bytes 9604
  16.3 30.4 %copy-start.32 = (f32[800]{0:T(1024)}, f32[800]{0:T(1024)S(1)}, u32[]{:S(2)}) copy-start(f32[800]{0:T(1024)S(1)} %get-tuple-element.70) | copy-start | bytes 9604
  16.3 30.4 %copy-start.34 = (f32[800]{0:T(1024)}, f32[800]{0:T(1024)S(1)}, u32[]{:S(2)}) copy-start(f32[800]{0:T(1024)S(1)} %get-tuple-element.71) | copy-start | bytes 9604
  16.3 30.4 %copy-start.36 = (f32[800]{0:T(1024)}, f32[800]{0:T(1024)S(1)}, u32[]{:S(2)}) copy-start(f32[800]{0:T(1024)S(1)} %get-tuple-element.72) | copy-start | bytes 9604
  16.3 30.4 %copy-start.38 = (f32[800]{0:T(1024)}, f32[800]{0:T(1024)S(1)}, u32[]{:S(2)}) copy-start(f32[800]{0:T(1024)S(1)} %get-tuple-element.73) | copy-start | bytes 9604
  16.4 30.4 %copy-start.40 = (f32[800]{0:T(1024)}, f32[800]{0:T(1024)S(1)}, u32[]{:S(2)}) copy-start(f32[800]{0:T(1024)S(1)} %get-tuple-element.74) | copy-start | bytes 9604
  16.4 30.4 %copy-start.42 = (f32[800]{0:T(1024)}, f32[800]{0:T(1024)S(1)}, u32[]{:S(2)}) copy-start(f32[800]{0:T(1024)S(1)} %get-tuple-element.75) | copy-start | bytes 9604
  16.4 30.4 %copy-start.44 = (f32[800]{0:T(1024)}, f32[800]{0:T(1024)S(1)}, u32[]{:S(2)}) copy-start(f32[800]{0:T(1024)S(1)} %get-tuple-element.76) | copy-start | bytes 9604
  16.6 30.2 %copy-start.46 = (f32[800]{0:T(1024)}, f32[800]{0:T(1024)S(1)}, u32[]{:S(2)}) copy-start(f32[800]{0:T(1024)S(1)} %get-tuple-element.77) | copy-start | bytes 9604
  16.6 30.2 %copy-start.48 = (f32[800]{0:T(1024)}, f32[800]{0:T(1024)S(1)}, u32[]{:S(2)}) copy-start(f32[800]{0:T(1024)S(1)} %get-tuple-element.78) | copy-start | bytes 9604
  16.6 30.2 %copy-start.50 = (f32[800]{0:T(1024)}, f32[800]{0:T(1024)S(1)}, u32[]{:S(2)}) copy-start(f32[800]{0:T(1024)S(1)} %get-tuple-element.79) | copy-start | bytes 9604
  16.6 30.2 %copy-start.52 = (f32[800]{0:T(1024)}, f32[800]{0:T(1024)S(1)}, u32[]{:S(2)}) copy-start(f32[800]{0:T(1024)S(1)} %get-tuple-element.80) | copy-start | bytes 9604
  16.6 30.2 %copy-start.54 = (f32[800]{0:T(1024)}, f32[800]{0:T(1024)S(1)}, u32[]{:S(2)}) copy-start(f32[800]{0:T(1024)S(1)} %get-tuple-element.81) | copy-start | bytes 9604
  16.6 30.2 %copy-start.56 = (f32[800]{0:T(1024)}, f32[800]{0:T(1024)S(1)}, u32[]{:S(2)}) copy-start(f32[800]{0:T(1024)S(1)} %get-tuple-element.82) | copy-start | bytes 9604
  16.6 30.2 %copy-start.58 = (f32[800]{0:T(1024)}, f32[800]{0:T(1024)S(1)}, u32[]{:S(2)}) copy-start(f32[800]{0:T(1024)S(1)} %get-tuple-element.83) | copy-start | bytes 9604
  16.7 30.2 %copy-start.60 = (f32[800]{0:T(1024)}, f32[800]{0:T(1024)S(1)}, u32[]{:S(2)}) copy-start(f32[800]{0:T(1024)S(1)} %get-tuple-element.84) | copy-start | bytes 9604
  16.7 30.2 %copy-start.62 = (f32[800]{0:T(1024)}, f32[800]{0:T(1024)S(1)}, u32[]{:S(2)}) copy-start(f32[800]{0:T(1024)S(1)} %get-tuple-element.85) | copy-start | bytes 9604
  16.7 30.2 %copy-start.64 = (f32[800]{0:T(1024)}, f32[800]{0:T(1024)S(1)}, u32[]{:S(2)}) copy-start(f32[800]{0:T(1024)S(1)} %get-tuple-element.86) | copy-start | bytes 9604
  16.7 30.2 %copy-start.66 = (f32[800]{0:T(1024)}, f32[800]{0:T(1024)S(1)}, u32[]{:S(2)}) copy-start(f32[800]{0:T(1024)S(1)} %get-tuple-element.87) | copy-start | bytes 9604
  16.7 30.2 %copy-start.68 = (f32[800]{0:T(1024)}, f32[800]{0:T(1024)S(1)}, u32[]{:S(2)}) copy-start(f32[800]{0:T(1024)S(1)} %get-tuple-element.88) | copy-start | bytes 9604
  16.7 30.2 %copy-start.70 = (f32[800]{0:T(1024)}, f32[800]{0:T(1024)S(1)}, u32[]{:S(2)}) copy-start(f32[800]{0:T(1024)S(1)} %get-tuple-element.89) | copy-start | bytes 9604
  16.7 30.2 %copy-start.72 = (f32[800]{0:T(1024)}, f32[800]{0:T(1024)S(1)}, u32[]{:S(2)}) copy-start(f32[800]{0:T(1024)S(1)} %get-tuple-element.90) | copy-start | bytes 9604
  16.7 30.2 %copy-start.74 = (f32[800]{0:T(1024)}, f32[800]{0:T(1024)S(1)}, u32[]{:S(2)}) copy-start(f32[800]{0:T(1024)S(1)} %get-tuple-element.91) | copy-start | bytes 9604
  16.7 30.2 %copy-start.76 = (f32[800]{0:T(1024)}, f32[800]{0:T(1024)S(1)}, u32[]{:S(2)}) copy-start(f32[800]{0:T(1024)S(1)} %get-tuple-element.92) | copy-start | bytes 9604
  34.7 6.4 collective-permute-start.3
  36.0 5.1 collective-permute-start.2
  47.0 130.6 %copy-start.2 = (bf16[4,8,32,800]{3,2,1,0:T(8,128)(2,1)S(1)}, bf16[4,8,32,800]{3,2,1,0:T(8,128)(2,1)}, u32[]{:S(2)}) copy-start(bf16[4,8,32,800]{3,2,1,0:T(8,128)(2,1)} %param.21) | copy-start | bytes 4915204
  314.7 36.2 %copy-start.88 = (f32[800]{0:T(1024)}, f32[800]{0:T(1024)S(1)}, u32[]{:S(2)}) copy-start(f32[800]{0:T(1024)S(1)} %get-tuple-element.145) | copy-start | bytes 9604
  314.7 36.2 %copy-start.89 = (f32[800]{0:T(1024)}, f32[800]{0:T(1024)S(1)}, u32[]{:S(2)}) copy-start(f32[800]{0:T(1024)S(1)} %get-tuple-element.146) | copy-start | bytes 9604
  373.7 40.0 %copy-start.6 = (bf16[4,8,32,800]{3,2,1,0:T(8,128)(2,1)S(1)}, bf16[4,8,32,800]{3,2,1,0:T(8,128)(2,1)}, u32[]{:S(2)}) copy-start(bf16[4,8,32,800]{3,2,1,0:T(8,128)(2,1)} %copy-done.5) | copy-start | bytes 4915204
  442.6 31.9 %collective-permute-start.5 = (bf16[4,3,32,800]{3,2,1,0:T(8,128)(2,1)}, bf16[4,3,32,800]{3,2,1,0:T(8,128)(2,1)S(1)}, u32[]{:S(2)}, u32[]{:S(2)}) collective-permute-start(bf16[4,3,32,800]{3,2,1,0:T(8,128)(2,1)} %get-tuple-element.132), channel_id=1, source_target_pairs={{8,0},{16,8},{24,16},{9,1},{17,9},{25,17},{10,2},{18,10},{26,18},{... | collective-permute-start | bytes 1843208 | tf_op jit(solution)/shard_map/ppermute | solution.py:19
  443.9 34.7 %collective-permute-start.4 = (bf16[4,3,32,800]{3,2,1,0:T(8,128)(2,1)}, bf16[4,3,32,800]{3,2,1,0:T(8,128)(2,1)S(1)}, u32[]{:S(2)}, u32[]{:S(2)}) collective-permute-start(bf16[4,3,32,800]{3,2,1,0:T(8,128)(2,1)} %get-tuple-element.131), channel_id=1, source_target_pairs={{0,8},{8,16},{16,24},{1,9},{9,17},{17,25},{2,10},{10,18},{18,26},{... | collective-permute-start | bytes 1843208 | tf_op jit(solution)/shard_map/ppermute | solution.py:18
  478.9 8.2 %collective-permute-start.7 = (bf16[4,14,3,800]{3,2,1,0:T(4,128)(2,1)S(1)}, bf16[4,14,3,800]{3,2,1,0:T(4,128)(2,1)S(1)}, u32[]{:S(2)}, u32[]{:S(2)}) collective-permute-start(bf16[4,14,3,800]{3,2,1,0:T(4,128)(2,1)S(1)} %get-tuple-element.127), channel_id=1, source_target_pairs={{1,0},{2,1},{3,2},{4,3},{5,4},{6,5},{7,6},{9,8},{10,9},{11,10},{12... | collective-permute-start | bytes 806408 | tf_op jit(solution)/shard_map/ppermute | solution.py:19
  480.2 6.9 collective-permute-start.6
  (61 other events, 499.1 us)
Sparse Core Ops, SparseCore 0:
  441.3 339.6 all-reduce.4
where the time goes:
time: 811 us; the launch traced here: 803 us
  other arithmetic  316 us (39%)
  waiting for transfers between devices  213 us (26%)
  blocking collectives  128 us (16%)
  matrix products  75.9 us (9%)
  local copies, waits for them, and re-layouts  32.5 us (4%)
  starting transfers between devices  20.9 us (3%)
  between operations  16.9 us (2%)
    psum x1, waiting for transfers between devices, body(): lax.psum((local_w_in, local_b_in, local_w_out, local_b_out, local_kernel)...  184 us
    convert_element_type x1, other arithmetic, body(): d_inputs.astype(jnp.bfloat16)  105 us
    reduce_sum x3, other arithmetic, body(): jnp.sum(padded[:, row_shift:row_shift + tile_rows, col_shift:col_shift +...  99 us
    reduce_sum x1, other arithmetic, body(): jnp.sum(masked, axis=(0, 1, 2))  83.2 us
    psum x1, blocking collectives, body(): lax.psum((jnp.sum(masked, axis=(0, 1, 2)), local_count), ('lat', 'lon'))  46.7 us
    psum x1, blocking collectives, body(): lax.psum((jnp.sum(d_normed, axis=(0, 1, 2)), jnp.sum(d_normed * standard,...  41.2 us
    psum x1, blocking collectives, body(): lax.psum(jnp.sum(centered * centered * ocean_cells, axis=(0, 1, 2)), ('la...  40 us
    unnamed x211, local copies, waits for them, and re-layouts  17.7 us
  transfers between devices with their start and end apart: 9, of which 5 were waited for; matrix products, arithmetic and copies ran while one was open for 17% of the time, Pallas kernels for 0%

commit v1 on v0

--- a/solution.py
+++ b/solution.py
@@ -57,7 +57,12 @@
     mean_value = sum_cells / cell_count
     centered = convolved - mean_value
     variance = (
-        lax.psum(jnp.sum(centered * centered * ocean_cells, axis=(0, 1, 2)), ("lat", "lon"))
+        jnp.sum(
+            lax.all_gather(
+                jnp.sum(centered * centered * ocean_cells, axis=(0, 1, 2)), ("lat", "lon")
+            ),
+            axis=0,
+        )
         / cell_count
     )
     inv_std = lax.rsqrt(variance + epsilon)

time: 811 us -> 895 us (1.10)
  waiting for transfers between devices: 213 us -> 337 us
  blocking collectives: 128 us -> 88.8 us
    unnamed x1 -> x3, waiting for transfers between devices: 0.02 us -> 123 us
    psum x1 -> x0, blocking collectives: 40 us -> none  [body(): lax.psum(jnp.sum(centered * centered * ocean_cells, axis=(0, 1, 2)), ('la...]
    unnamed x211 -> x215, local copies, waits for them, and re-layouts: 17.7 us -> 18.7 us
  transfers between devices with their start and end apart: 9 -> 10, of which waited for: 5 -> 6; matrix products, arithmetic and copies ran while one was open for 17% -> 15% of each run, Pallas kernels for 0% -> 0%
where the time goes in v1:
time: 895 us; the launch traced here: 887 us
  waiting for transfers between devices  337 us (38%)
  other arithmetic  316 us (35%)
  blocking collectives  88.8 us (10%)
  matrix products  74.7 us (8%)
  local copies, waits for them, and re-layouts  32.9 us (4%)
  starting transfers between devices  21.1 us (2%)
  between operations  17 us (2%)
    psum x1, waiting for transfers between devices, body(): lax.psum((local_w_in, local_b_in, local_w_out, local_b_out, local_kernel)...  185 us
    unnamed x3, waiting for transfers between devices  123 us
    convert_element_type x1, other arithmetic, body(): d_inputs.astype(jnp.bfloat16)  105 us
    reduce_sum x3, other arithmetic, body(): jnp.sum(padded[:, row_shift:row_shift + tile_rows, col_shift:col_shift +...  99 us
    reduce_sum x1, other arithmetic, body(): jnp.sum(masked, axis=(0, 1, 2))  83.2 us
    psum x1, blocking collectives, body(): lax.psum((jnp.sum(masked, axis=(0, 1, 2)), local_count), ('lat', 'lon'))  46.7 us
    psum x1, blocking collectives, body(): lax.psum((jnp.sum(d_normed, axis=(0, 1, 2)), jnp.sum(d_normed * standard,...  42.1 us
    unnamed x215, local copies, waits for them, and re-layouts  18.7 us
  transfers between devices with their start and end apart: 10, of which 6 were waited for; matrix products, arithmetic and copies ran while one was open for 15% of the time, Pallas kernels for 0%

profile of v1, /device:TPU:0, one launch (start us, length us, event | category | flops | bytes accessed | tf_op | source)
XLA Modules:
  0.0 887.3 jit_solution(9346815738429483507)
XLA Ops:
  7.2 1.5 fusion.116
  8.8 5.0 collective-permute-start
  13.8 1.3 collective-permute-start.1
  15.1 0.9 convert_element_type.65
  16.8 1.4 fusion.117
  18.2 10.2 %collective-permute-done = bf16[4,3,32,800]{3,2,1,0:T(8,128)(2,1)S(1)} collective-permute-done((bf16[4,3,32,800]{3,2,1,0:T(8,128)(2,1)S(1)}, bf16[4,3,32,800]{3,2,1,0:T(8,128)(2,1)S(1)}, u32[]{:S(2)}, u32[]{:S(2)}) %collective-permute-start) | collective-permute-done | bytes 614432 | tf_op jit(solution)/shard_map/ppermute | solution.py:18
  28.8 3.7 collective-permute-done.1
  32.7 1.7 copy-done.3
  34.7 1.3 collective-permute-start.3
  36.0 3.1 collective-permute-start.2
  39.1 0.7 slice_reduce_fusion.46
  41.0 5.5 maximum_convert_fusion
  46.9 83.2 %multiply_reduce_fusion.2 = (f32[800]{0:T(1024)S(1)}, f32[4,8,32,800]{3,2,1,0:T(8,128)}) fusion(f32[8,32]{1,0:T(8,128)S(1)} %get-tuple-element.136, f32[4,14,38,800]{3,2,1,0:T(8,128)} %maximum_convert_fusion, f32[800]{0:T(1024)S(1)} %get-tuple-element.59, f32[800]{0:T(1024)S(1)} %get-tuple-element.60, f32[800]{0:T(1024)S(1)} %get-tuple-element.61, ...), kind=kLoop, calls=%fused_computation.217 | loop fusion | flops 81100000 | bytes 164001024 | tf_op jit(solution)/shard_map/reduce_sum | solution.py:56
  130.2 46.7 %all-reduce.2 = (f32[800]{0:T(1024)S(1)}, f32[]{:T(128)}) all-reduce(f32[800]{0:T(1024)S(1)} %get-tuple-element.123, f32[]{:T(128)S(6)} %mul.1208), channel_id=1, replica_groups=mesh['lat'=4,'lon'=8] {'lat','lon'}, use_global_device_ids=true, to_apply=%region_1.0 | all-reduce | flops 801 | bytes 6408 | tf_op jit(solution)/shard_map/psum | solution.py:56
  176.9 0.7 broadcast_divide_fusion
  177.7 4.4 fusion.106
  183.3 123.4 %all-reduce.7.cloned.1.call-done = f32[25600]{0:T(1024)} async-done(((f32[25600]{0:T(1024)}), f32[25600]{0:T(1024)}) %all-reduce.7.cloned.1.call-update) | async-done | bytes 102416
  306.8 1.0 reshape.96
  307.8 0.7 convert_multiply_fusion.50
  308.5 2.8 add_convert_fusion.1
  311.3 13.3 %fusion.119 = f32[1024,3200]{1,0:T(8,128)} fusion(bf16[1024,800]{1,0:T(8,128)(2,1)S(1)} %bitcast.38, bf16[800,3200]{1,0:T(8,128)(2,1)} %param.15), kind=kOutput, calls=%fused_computation.297 | convolution fusion | flops 5242880000 | bytes 19865600 | tf_op jit(solution)/shard_map/dot_general | solution.py:76
  324.6 16.9 %fusion.112 = (f32[3200]{0:T(1024)S(1)}, bf16[1024,3200]{1,0:T(8,128)(2,1)}, bf16[1024,3200]{1,0:T(8,128)(2,1)}) fusion(f32[1024,3200]{1,0:T(8,128)} %fusion.119, f32[3200]{0:T(1024)S(1)} %convert_element_type.71, bf16[1024,800]{1,0:T(8,128)(2,1)S(1)} %bitcast.37, bf16[3200,800]{0,1:T(8,128)(2,1)S(1)} %bitcast.43), kind=kOutput, calls=%fused_computation.291 | convolution fusion | flops 5321520128 | bytes 32998400 | tf_op jit(solution)/shard_map/dot_general | solution.py:91
  341.5 8.0 fusion.118
  349.6 3.3 copy.26
  352.9 3.8 multiply_reduce_fusion
  356.6 42.1 %all-reduce.1 = (f32[800]{0:T(1024)S(1)}, f32[800]{0:T(1024)S(1)}, f32[3200]{0:T(1024)}, f32[800]{0:T(1024)}) all-reduce(f32[800]{0:T(1024)S(1)} %multiply_reduce_fusion, f32[800]{0:T(1024)S(1)} %get-tuple-element.137, f32[3200]{0:T(1024)S(1)} %get-tuple-element.121, ...), channel_id=1, replica_groups=mesh['lat'=4,'lon'=8] {'lat','lon'}, use_global_device_ids=true, to_apply=%region_9.0 | all-reduce | flops 5600 | bytes 44800 | tf_op jit(solution)/shard_map/psum | solution.py:103
  398.7 36.3 %fusion.53 = (f32[800]{0:T(1024)S(1)}, f32[800]{0:T(1024)S(1)}, f32[800]{0:T(1024)S(1)}, f32[800]{0:T(1024)S(1)}, f32[800]{0:T(1024)S(1)}, /*index=5*/f32[800]{0...) fusion(f32[4,14,38,800]{3,2,1,0:T(8,128)} %maximum_convert_fusi, ...), kind=kLoop, calls=%fused_computation.107 | loop fusion | flops 37668800 | bytes 67249024 | tf_op jit(solution)/shard_map/reduce_sum | solution.py:126
  435.0 22.8 %fusion.52 = (f32[800]{0:T(1024)S(1)}, f32[800]{0:T(1024)S(1)}, f32[800]{0:T(1024)S(1)}, f32[800]{0:T(1024)S(1)}, f32[800]{0:T(1024)S(1)}, /*index=5*/f32[800]{0...) fusion(bf16[4,8,32,800]{3,2,1,0:T(8,128)(2,1)S(1)} %get-tuple-e, ...), kind=kLoop, calls=%fused_computation.106 | loop fusion | flops 22108000 | bytes 44278400 | tf_op jit(solution)/shard_map/reduce_sum | solution.py:126
  457.8 40.0 %fusion.54 = (f32[800]{0:T(1024)S(1)}, f32[800]{0:T(1024)S(1)}, f32[800]{0:T(1024)S(1)}, f32[800]{0:T(1024)S(1)}, f32[800]{0:T(1024)S(1)}, /*index=5*/f32[800]{0...) fusion(bf16[4,8,32,800]{3,2,1,0:T(8,128)(2,1)S(1)} %get-tuple-e, ...), kind=kLoop, calls=%fused_computation.108 | loop fusion | flops 30296000 | bytes 60678400 | tf_op jit(solution)/shard_map/reduce_sum | solution.py:126
  497.8 12.6 %fusion.108 = f32[800,3200]{1,0:T(8,128)} fusion(bf16[1024,800]{1,0:T(8,128)(2,1)S(1)} %bitcast.39, bf16[1024,3200]{1,0:T(8,128)(2,1)} %get-tuple-element.122), kind=kOutput, calls=%fused_computation.220 | convolution fusion | flops 5242880000 | bytes 18432000 | tf_op jit(solution)/shard_map/dot_general | solution.py:97
  511.1 13.1 %fusion.120 = f32[3200,800]{0,1:T(8,128)} fusion(bf16[1024,3200]{1,0:T(8,128)(2,1)} %get-tuple-element.125, bf16[1024,800]{1,0:T(8,128)(2,1)} %bitcast.36), kind=kOutput, calls=%fused_computation.298 | convolution fusion | flops 5242880000 | bytes 18432000 | tf_op jit(solution)/shard_map/dot_general | solution.py:88
  524.6 0.7 copy-done.8
  525.3 1.4 fusion.115
  526.7 1.3 collective-permute-start.5
  528.0 4.6 collective-permute-start.4
  532.6 10.9 %convolution_add_fusion = f32[1024,800]{0,1:T(8,128)} fusion(bf16[1024,3200]{1,0:T(8,128)(2,1)} %get-tuple-element.125, bf16[3200,800]{0,1:T(8,128)(2,1)} %param.17, f32[800]{0:T(1024)S(1)} %convert_element_type.73), kind=kOutput, calls=%fused_computation.224 | convolution fusion | flops 5243699200 | bytes 14953600 | tf_op jit(solution)/shard_map/dot_general | solution.py:79
  543.4 4.9 copy.25
  548.4 10.9 %collective-permute-done.5 = bf16[4,3,32,800]{3,2,1,0:T(8,128)(2,1)S(1)} collective-permute-done((bf16[4,3,32,800]{3,2,1,0:T(8,128)(2,1)}, bf16[4,3,32,800]{3,2,1,0:T(8,128)(2,1)S(1)}, u32[]{:S(2)}, u32[]{:S(2)}) %collective-permute-start.5) | collective-permute-done | bytes 614432 | tf_op jit(solution)/shard_map/ppermute | solution.py:19
  559.2 3.4 collective-permute-done.4
  563.0 1.3 collective-permute-start.7
  564.3 3.1 collective-permute-start.6
  567.3 3.4 add_convert_fusion
  571.2 4.2 maximum_convert_fusion.1
  575.8 104.8 %fusion.56 = bf16[4,8,32,800]{3,2,1,0:T(8,128)(2,1)} fusion(f32[4,14,38,800]{3,2,1,0:T(8,128)} %maximum_convert_fusion.1, bf16[4,8,32,800]{3,2,1,0:T(8,128)(2,1)} %param.21, f32[4]{0:T(128)} %convert_multiply_fusion.51, f32[800]{0:T(1024)S(1)} %copy-done.12, f32[800]{0:T(1024)S(1)} %copy-done.14, f32[800]{0:T(1024)S(1)} %copy-done.16, ...), kind=kLoop, calls=%fused_computation.111 | loop fusion | flops 82739200 | bytes 163996816 | tf_op jit(solution)/shard_map/convert_element_type | solution.py:139
  680.6 185.1 %all-reduce.9.cloned.1.call-done = (f32[7,7,800]{2,1,0:T(8,128)}, f32[800,3200]{1,0:T(8,128)}, f32[3200,800]{0,1:T(8,128)}) async-done(((f32[7,7,800]{2,1,0:T(8,128)}, f32[800,3200]{1,0:T(8,128)}, f32[3200,800]{0,1:T(8,128)}), (f32[7,7,800]{2,1,0:T(8,128)}, f32[800,3200]{1,0:T(8,128)}, f32[3200,800]{0,1:T(8,128)})) %all-reduce.9.cloned.1.call-update) | async-done | bytes 20636816 | tf_op jit(solution)/shard_map/psum | solution.py:134
  865.7 1.8 copy.40
  867.5 8.7 copy.41
  876.3 4.0 copy.42
  (289 shorter events, 4.4 us)
Async XLA Ops:
  7.2 299.6 %all-reduce.7.cloned.1.call-start = ((), (), s32[]{:S(2)}) async-start(), calls=%async_computation | async-start | bytes 204800
  8.8 19.6 %collective-permute-start = (bf16[4,3,32,800]{3,2,1,0:T(8,128)(2,1)S(1)}, bf16[4,3,32,800]{3,2,1,0:T(8,128)(2,1)S(1)}, u32[]{:S(2)}, u32[]{:S(2)}) collective-permute-start(bf16[4,3,32,800]{3,2,1,0:T(8,128)(2,1)S(1)} %get-tuple-element.134), channel_id=1, source_target_pairs={{0,8},{8,16},{16,24},{1,9},{9,17},{17,25},{2,10},{10,18},{18,26},{... | collective-permute-start | bytes 1843208 | tf_op jit(solution)/shard_map/ppermute | solution.py:18
  13.8 18.8 %collective-permute-start.1 = (bf16[4,3,32,800]{3,2,1,0:T(8,128)(2,1)S(1)}, bf16[4,3,32,800]{3,2,1,0:T(8,128)(2,1)S(1)}, u32[]{:S(2)}, u32[]{:S(2)}) collective-permute-start(bf16[4,3,32,800]{3,2,1,0:T(8,128)(2,1)S(1)} %get-tuple-element.133), channel_id=1, source_target_pairs={{8,0},{16,8},{24,16},{9,1},{17,9},{25,17},{10,2},{18,10},{26,18},{... | collective-permute-start | bytes 1843208 | tf_op jit(solution)/shard_map/ppermute | solution.py:19
  16.2 30.3 %copy-start.9 = (f32[800]{0:T(1024)}, f32[800]{0:T(1024)S(1)}, u32[]{:S(2)}) copy-start(f32[800]{0:T(1024)S(1)} %get-tuple-element.58) | copy-start | bytes 9604
  16.2 30.3 %copy-start.11 = (f32[800]{0:T(1024)}, f32[800]{0:T(1024)S(1)}, u32[]{:S(2)}) copy-start(f32[800]{0:T(1024)S(1)} %get-tuple-element.59) | copy-start | bytes 9604
  16.2 30.3 %copy-start.13 = (f32[800]{0:T(1024)}, f32[800]{0:T(1024)S(1)}, u32[]{:S(2)}) copy-start(f32[800]{0:T(1024)S(1)} %get-tuple-element.60) | copy-start | bytes 9604
  16.2 30.3 %copy-start.15 = (f32[800]{0:T(1024)}, f32[800]{0:T(1024)S(1)}, u32[]{:S(2)}) copy-start(f32[800]{0:T(1024)S(1)} %get-tuple-element.61) | copy-start | bytes 9604
  16.2 30.3 %copy-start.17 = (f32[800]{0:T(1024)}, f32[800]{0:T(1024)S(1)}, u32[]{:S(2)}) copy-start(f32[800]{0:T(1024)S(1)} %get-tuple-element.62) | copy-start | bytes 9604
  16.2 30.3 %copy-start.19 = (f32[800]{0:T(1024)}, f32[800]{0:T(1024)S(1)}, u32[]{:S(2)}) copy-start(f32[800]{0:T(1024)S(1)} %get-tuple-element.63) | copy-start | bytes 9604
  16.3 30.3 %copy-start.21 = (f32[800]{0:T(1024)}, f32[800]{0:T(1024)S(1)}, u32[]{:S(2)}) copy-start(f32[800]{0:T(1024)S(1)} %get-tuple-element.64) | copy-start | bytes 9604
  16.3 30.3 %copy-start.23 = (f32[800]{0:T(1024)}, f32[800]{0:T(1024)S(1)}, u32[]{:S(2)}) copy-start(f32[800]{0:T(1024)S(1)} %get-tuple-element.65) | copy-start | bytes 9604
  16.3 30.3 %copy-start.25 = (f32[800]{0:T(1024)}, f32[800]{0:T(1024)S(1)}, u32[]{:S(2)}) copy-start(f32[800]{0:T(1024)S(1)} %get-tuple-element.66) | copy-start | bytes 9604
  16.3 30.3 %copy-start.27 = (f32[800]{0:T(1024)}, f32[800]{0:T(1024)S(1)}, u32[]{:S(2)}) copy-start(f32[800]{0:T(1024)S(1)} %get-tuple-element.67) | copy-start | bytes 9604
  16.3 30.3 %copy-start.29 = (f32[800]{0:T(1024)}, f32[800]{0:T(1024)S(1)}, u32[]{:S(2)}) copy-start(f32[800]{0:T(1024)S(1)} %get-tuple-element.68) | copy-start | bytes 9604
  16.3 30.3 %copy-start.31 = (f32[800]{0:T(1024)}, f32[800]{0:T(1024)S(1)}, u32[]{:S(2)}) copy-start(f32[800]{0:T(1024)S(1)} %get-tuple-element.69) | copy-start | bytes 9604
  16.3 30.3 %copy-start.33 = (f32[800]{0:T(1024)}, f32[800]{0:T(1024)S(1)}, u32[]{:S(2)}) copy-start(f32[800]{0:T(1024)S(1)} %get-tuple-element.70) | copy-start | bytes 9604
  16.3 30.3 %copy-start.35 = (f32[800]{0:T(1024)}, f32[800]{0:T(1024)S(1)}, u32[]{:S(2)}) copy-start(f32[800]{0:T(1024)S(1)} %get-tuple-element.71) | copy-start | bytes 9604
  16.3 30.3 %copy-start.37 = (f32[800]{0:T(1024)}, f32[800]{0:T(1024)S(1)}, u32[]{:S(2)}) copy-start(f32[800]{0:T(1024)S(1)} %get-tuple-element.72) | copy-start | bytes 9604
  16.3 30.3 %copy-start.39 = (f32[800]{0:T(1024)}, f32[800]{0:T(1024)S(1)}, u32[]{:S(2)}) copy-start(f32[800]{0:T(1024)S(1)} %get-tuple-element.73) | copy-start | bytes 9604
  16.4 30.3 %copy-start.41 = (f32[800]{0:T(1024)}, f32[800]{0:T(1024)S(1)}, u32[]{:S(2)}) copy-start(f32[800]{0:T(1024)S(1)} %get-tuple-element.74) | copy-start | bytes 9604
  16.4 30.3 %copy-start.43 = (f32[800]{0:T(1024)}, f32[800]{0:T(1024)S(1)}, u32[]{:S(2)}) copy-start(f32[800]{0:T(1024)S(1)} %get-tuple-element.75) | copy-start | bytes 9604
  16.4 30.3 %copy-start.45 = (f32[800]{0:T(1024)}, f32[800]{0:T(1024)S(1)}, u32[]{:S(2)}) copy-start(f32[800]{0:T(1024)S(1)} %get-tuple-element.76) | copy-start | bytes 9604
  16.6 30.1 %copy-start.47 = (f32[800]{0:T(1024)}, f32[800]{0:T(1024)S(1)}, u32[]{:S(2)}) copy-start(f32[800]{0:T(1024)S(1)} %get-tuple-element.77) | copy-start | bytes 9604
  16.6 30.1 %copy-start.49 = (f32[800]{0:T(1024)}, f32[800]{0:T(1024)S(1)}, u32[]{:S(2)}) copy-start(f32[800]{0:T(1024)S(1)} %get-tuple-element.78) | copy-start | bytes 9604
  16.6 30.1 %copy-start.51 = (f32[800]{0:T(1024)}, f32[800]{0:T(1024)S(1)}, u32[]{:S(2)}) copy-start(f32[800]{0:T(1024)S(1)} %get-tuple-element.79) | copy-start | bytes 9604
  16.6 30.1 %copy-start.53 = (f32[800]{0:T(1024)}, f32[800]{0:T(1024)S(1)}, u32[]{:S(2)}) copy-start(f32[800]{0:T(1024)S(1)} %get-tuple-element.80) | copy-start | bytes 9604
  16.6 30.1 %copy-start.55 = (f32[800]{0:T(1024)}, f32[800]{0:T(1024)S(1)}, u32[]{:S(2)}) copy-start(f32[800]{0:T(1024)S(1)} %get-tuple-element.81) | copy-start | bytes 9604
  16.6 30.1 %copy-start.57 = (f32[800]{0:T(1024)}, f32[800]{0:T(1024)S(1)}, u32[]{:S(2)}) copy-start(f32[800]{0:T(1024)S(1)} %get-tuple-element.82) | copy-start | bytes 9604
  16.6 30.1 %copy-start.59 = (f32[800]{0:T(1024)}, f32[800]{0:T(1024)S(1)}, u32[]{:S(2)}) copy-start(f32[800]{0:T(1024)S(1)} %get-tuple-element.83) | copy-start | bytes 9604
  16.7 30.1 %copy-start.61 = (f32[800]{0:T(1024)}, f32[800]{0:T(1024)S(1)}, u32[]{:S(2)}) copy-start(f32[800]{0:T(1024)S(1)} %get-tuple-element.84) | copy-start | bytes 9604
  16.7 30.1 %copy-start.63 = (f32[800]{0:T(1024)}, f32[800]{0:T(1024)S(1)}, u32[]{:S(2)}) copy-start(f32[800]{0:T(1024)S(1)} %get-tuple-element.85) | copy-start | bytes 9604
  16.7 30.1 %copy-start.65 = (f32[800]{0:T(1024)}, f32[800]{0:T(1024)S(1)}, u32[]{:S(2)}) copy-start(f32[800]{0:T(1024)S(1)} %get-tuple-element.86) | copy-start | bytes 9604
  16.7 30.1 %copy-start.67 = (f32[800]{0:T(1024)}, f32[800]{0:T(1024)S(1)}, u32[]{:S(2)}) copy-start(f32[800]{0:T(1024)S(1)} %get-tuple-element.87) | copy-start | bytes 9604
  16.7 30.1 %copy-start.69 = (f32[800]{0:T(1024)}, f32[800]{0:T(1024)S(1)}, u32[]{:S(2)}) copy-start(f32[800]{0:T(1024)S(1)} %get-tuple-element.88) | copy-start | bytes 9604
  16.7 30.1 %copy-start.71 = (f32[800]{0:T(1024)}, f32[800]{0:T(1024)S(1)}, u32[]{:S(2)}) copy-start(f32[800]{0:T(1024)S(1)} %get-tuple-element.89) | copy-start | bytes 9604
  16.7 30.1 %copy-start.73 = (f32[800]{0:T(1024)}, f32[800]{0:T(1024)S(1)}, u32[]{:S(2)}) copy-start(f32[800]{0:T(1024)S(1)} %get-tuple-element.90) | copy-start | bytes 9604
  34.7 6.3 collective-permute-start.3
  36.0 5.0 collective-permute-start.2
  46.9 130.7 %copy-start.2 = (bf16[4,8,32,800]{3,2,1,0:T(8,128)(2,1)S(1)}, bf16[4,8,32,800]{3,2,1,0:T(8,128)(2,1)}, u32[]{:S(2)}) copy-start(bf16[4,8,32,800]{3,2,1,0:T(8,128)(2,1)} %param.21) | copy-start | bytes 4915204
  183.1 682.7 %all-reduce.9.cloned.1.call-start = ((), (), s32[]{:S(2)}) async-start(), calls=%async_computation.1 | async-start | bytes 41361408 | tf_op jit(solution)/shard_map/psum | solution.py:134
  311.3 30.2 %slice-start.3 = ((s8[5120000]{0:T(1024)(128)(4,1)}), s8[4194304]{0:T(1024)(128)(4,1)S(1)}, s32[]{:S(2)}) async-start(s8[5120000]{0:T(1024)(128)(4,1)} %bitcast.40), calls=%async_computation.5 | async-start | bytes 8388608
  398.7 36.3 %copy-start.89 = (f32[800]{0:T(1024)}, f32[800]{0:T(1024)S(1)}, u32[]{:S(2)}) copy-start(f32[800]{0:T(1024)S(1)} %get-tuple-element.145) | copy-start | bytes 9604
  398.7 36.3 %copy-start.90 = (f32[800]{0:T(1024)}, f32[800]{0:T(1024)S(1)}, u32[]{:S(2)}) copy-start(f32[800]{0:T(1024)S(1)} %get-tuple-element.146) | copy-start | bytes 9604
  457.8 40.0 %copy-start.6 = (bf16[4,8,32,800]{3,2,1,0:T(8,128)(2,1)S(1)}, bf16[4,8,32,800]{3,2,1,0:T(8,128)(2,1)}, u32[]{:S(2)}) copy-start(bf16[4,8,32,800]{3,2,1,0:T(8,128)(2,1)} %copy-done.5) | copy-start | bytes 4915204
  526.7 32.5 %collective-permute-start.5 = (bf16[4,3,32,800]{3,2,1,0:T(8,128)(2,1)}, bf16[4,3,32,800]{3,2,1,0:T(8,128)(2,1)S(1)}, u32[]{:S(2)}, u32[]{:S(2)}) collective-permute-start(bf16[4,3,32,800]{3,2,1,0:T(8,128)(2,1)} %get-tuple-element.132), channel_id=1, source_target_pairs={{8,0},{16,8},{24,16},{9,1},{17,9},{25,17},{10,2},{18,10},{26,18},{... | collective-permute-start | bytes 1843208 | tf_op jit(solution)/shard_map/ppermute | solution.py:19
  528.0 34.7 %collective-permute-start.4 = (bf16[4,3,32,800]{3,2,1,0:T(8,128)(2,1)}, bf16[4,3,32,800]{3,2,1,0:T(8,128)(2,1)S(1)}, u32[]{:S(2)}, u32[]{:S(2)}) collective-permute-start(bf16[4,3,32,800]{3,2,1,0:T(8,128)(2,1)} %get-tuple-element.131), channel_id=1, source_target_pairs={{0,8},{8,16},{16,24},{1,9},{9,17},{17,25},{2,10},{10,18},{18,26},{... | collective-permute-start | bytes 1843208 | tf_op jit(solution)/shard_map/ppermute | solution.py:18
  563.0 8.2 collective-permute-start.7
  564.3 6.9 collective-permute-start.6
  (63 other events, 512.5 us)
Sparse Core Ops, SparseCore 0:
  183.2 123.5 all-reduce.6
  525.4 340.3 all-reduce.8
